TPU v7x, 32 devices: a whole 2x2x4 slice. The times are simulated.
32 devices in a mesh: section: 2 (over x), dp: 8 (over z, y), mp: 2 (over core).
Axes of the slice: x: 2, y: 2, z: 4, core: 2. Of those that a mesh axis runs over, the one named last changes fastest.
Arguments:
- layer_inputs: bfloat16 [2, 128, 4096], P('section', None, 'mp'), may hold values from -6 to 6
- pre_act: bfloat16 [2, 128, 8192], P('section', None, 'dp'), may hold values from -6 to 6
- out_grad: bfloat16 [128, 4096], P(None, 'mp'), may hold values from -4 to 4
- w_in: bfloat16 [8, 2, 512, 4096], P('dp', 'section', None, 'mp'), may hold values from -0.09375 to 0.09375
- w_out: bfloat16 [8, 2, 512, 4096], P('dp', 'section', None, 'mp'), may hold values from -0.0625 to 0.0625
Outputs:
- in_grads: bfloat16 [2, 128, 4096], P('section', None, 'mp')
- grad_in: float32 [8, 2, 512, 4096], P('dp', 'section', None, 'mp')
- grad_out: float32 [8, 2, 512, 4096], P('dp', 'section', None, 'mp')
All inputs are finite; a program needn't handle non-finite values.
Results may differ from a plain program's by a relative error of at most 0.035.
Values may be sent and summed in bfloat16 or wider, within the bound.
A program may use at most 64 MiB of HBM per device.

v0:
```python
import jax
import jax.numpy as jnp
from jax import lax
from jax.sharding import PartitionSpec as P

MICRO = 2


def shifted(value, axis, by):
    size = lax.axis_size(axis)
    pairs = [(i, i + by) for i in range(size) if 0 <= i + by < size]
    return lax.ppermute(value, axis, pairs)


def gelu_slope(value):
    cdf = 0.5 * (1.0 + lax.erf(value * 0.7071067811865476))
    dens = jnp.exp(-0.5 * value * value) * 0.3989422804014327
    return cdf + value * dens


def rounded(value):
    return lax.optimization_barrier(value.astype(jnp.bfloat16)).astype(jnp.float32)


def by_tokens(left, right):
    return lax.dot_general(
        left, right, (((0,), (0,)), ((), ())), preferred_element_type=jnp.float32
    )


def body(layer_inputs, pre_act, out_grad, w_in, w_out):
    sections = lax.axis_size("section")
    spot = lax.axis_index("section")
    tok_rows = out_grad.shape[0]
    block = tok_rows // MICRO
    width = out_grad.shape[1]
    full_in, full_out = (
        lax.all_gather(w_in, "section", axis=1, tiled=True),
        lax.all_gather(w_out, "section", axis=1, tiled=True),
    )
    units = full_in.shape[1] * full_in.shape[2]
    per_block = full_in.shape[2]
    in_rows = full_in.reshape(units, width)
    out_rows = full_out.reshape(units, width)
    inputs = layer_inputs[0]
    saved = pre_act[0]
    is_last = spot == sections - 1

    def advance(step, state):
        incoming, dys, gees, results = state
        micro_id = step - (sections - 1 - spot)
        valid = jnp.logical_and(micro_id >= 0, micro_id < MICRO)
        begin = jnp.clip(micro_id, 0, MICRO - 1) * block
        given = lax.dynamic_slice_in_dim(out_grad, begin, block, 0)
        upper = jnp.where(is_last, given, incoming)
        partial_value = lax.dot_general(
            upper, out_rows, (((1,), (1,)), ((), ())), preferred_element_type=jnp.float32
        )
        summed = lax.psum(partial_value.astype(jnp.bfloat16), "mp").astype(jnp.float32)
        rows_pre = lax.dynamic_slice_in_dim(saved, begin, block, 0).astype(jnp.float32)
        gee = (summed * gelu_slope(rows_pre)).astype(jnp.bfloat16)
        branch = jnp.dot(gee, in_rows, preferred_element_type=jnp.float32)
        total = lax.psum(branch.astype(jnp.bfloat16), "dp").astype(jnp.float32)
        result = (upper.astype(jnp.float32) + total).astype(jnp.bfloat16)
        outgoing = shifted(result, "section", -1)
        old_dy = lax.dynamic_slice_in_dim(dys, begin, block, 0)
        old_gee = lax.dynamic_slice_in_dim(gees, begin, block, 0)
        old_res = lax.dynamic_slice_in_dim(results, begin, block, 0)
        dys = lax.dynamic_update_slice_in_dim(dys, jnp.where(valid, upper, old_dy), begin, 0)
        gees = lax.dynamic_update_slice_in_dim(gees, jnp.where(valid, gee, old_gee), begin, 0)
        results = lax.dynamic_update_slice_in_dim(
            results, jnp.where(valid, result, old_res), begin, 0
        )
        return (outgoing, dys, gees, results)

    start_state = (
        jnp.zeros((block, width), jnp.bfloat16),
        jnp.zeros((tok_rows, width), jnp.bfloat16),
        jnp.zeros((tok_rows, units), jnp.bfloat16),
        jnp.zeros((tok_rows, width), jnp.bfloat16),
    )
    final_state = lax.fori_loop(0, sections + MICRO - 1, advance, start_state)
    dys = final_state[1]
    gees = final_state[2]
    results = final_state[3]
    hidden = jax.nn.gelu(saved.astype(jnp.float32), approximate=False).astype(jnp.bfloat16)
    offset = spot * per_block
    empty = jnp.zeros((per_block, width), jnp.float32)
    piece = (
        lax.all_gather(inputs[None], "section", axis=0, tiled=True),
        lax.all_gather(dys[None], "section", axis=0, tiled=True),
        lax.all_gather(gees[None], "section", axis=0, tiled=True),
        lax.all_gather(hidden[None], "section", axis=0, tiled=True),
    )
    acc_in = empty
    acc_out = empty
    for row in range(piece[0].shape[0]):
        gee_cols = lax.dynamic_slice_in_dim(piece[2][row], offset, per_block, 1)
        hid_cols = lax.dynamic_slice_in_dim(piece[3][row], offset, per_block, 1)
        acc_in = acc_in + rounded(by_tokens(gee_cols, piece[0][row]))
        acc_out = acc_out + rounded(by_tokens(hid_cols, piece[1][row]))
    acc_in, acc_out = (acc_in, acc_out)
    grad_in = acc_in.reshape(1, 1, per_block, width)
    grad_out = acc_out.reshape(1, 1, per_block, width)
    return (results[None], grad_in, grad_out)


def solution(mesh):
    in_specs = (
        P("section", None, "mp"),
        P("section", None, "dp"),
        P(None, "mp"),
        P("dp", "section", None, "mp"),
        P("dp", "section", None, "mp"),
    )
    out_specs = (
        P("section", None, "mp"),
        P("dp", "section", None, "mp"),
        P("dp", "section", None, "mp"),
    )
    return jax.shard_map(body, mesh=mesh, in_specs=in_specs, out_specs=out_specs, check_vma=False)
```

profile of v0, /device:TPU:0, one launch (start us, length us, event | category | flops | bytes accessed | tf_op | source)
XLA Modules:
  0.0 509.6 jit_solution(17135875296356808804)
XLA Ops:
  8.7 60.3 %all-gather.7.cloned.1.call-done = bf16[1,2,512,2048]{3,2,0,1:T(8,128)(2,1)} async-done(((bf16[1,1,512,2048]{3,2,0,1:T(8,128)(2,1)}), bf16[1,2,512,2048]{3,2,0,1:T(8,128)(2,1)}) %all-gather.7.cloned.1.call-update) | async-done | bytes 4194320 | tf_op jit(solution)/shard_map/all_gather | solution.py:39
  69.0 58.3 %all-gather.9.cloned.1.call-done = bf16[1,2,512,2048]{3,2,0,1:T(8,128)(2,1)} async-done(((bf16[1,1,512,2048]{3,2,0,1:T(8,128)(2,1)}), bf16[1,2,512,2048]{3,2,0,1:T(8,128)(2,1)}) %all-gather.9.cloned.1.call-update) | async-done | bytes 4194320 | tf_op jit(solution)/shard_map/all_gather | solution.py:38
  127.5 320.8 %while.21 = (s32[]{:T(128)}, bf16[64,2048]{1,0:T(8,128)(2,1)S(1)}, bf16[128,2048]{1,0:T(8,128)(2,1)S(1)}, bf16[128,1024]{1,0:T(8,128)(2,1)S(1)}, bf16[128,2048]{...) while((s32[]{:T(128)}, bf16[64,2048]{1,0:T(8,128)(2,1)S(1)}, ...), condition=%wide.region_3.4_spmd, body=%wide.region_0.3_spmd.sunk | while | flops 539820032 | bytes 16384420 | solution.py:82
  127.7 4.2 convolution_convert_fusion.8
  132.0 18.0 %all-reduce.3.cloned.1.call-done = bf16[64,1024]{1,0:T(8,128)(2,1)} async-done(((bf16[64,1024]{1,0:T(8,128)(2,1)}), bf16[64,1024]{1,0:T(8,128)(2,1)}) %all-reduce.3.cloned.1.call-update) | async-done | bytes 131088 | tf_op jit(solution)/shard_map/while/body/eval_jaxpr/psum | solution.py:59
  150.0 3.9 convolution_convert_fusion.9
  153.9 72.4 %all-reduce.5.cloned.1.call-done = bf16[64,2048]{1,0:T(8,128)(2,1)} async-done(((bf16[64,2048]{1,0:T(8,128)(2,1)}), bf16[64,2048]{1,0:T(8,128)(2,1)}) %all-reduce.5.cloned.1.call-update) | async-done | bytes 262160 | tf_op jit(solution)/shard_map/while/body/eval_jaxpr/psum | solution.py:63
  227.3 1.3 collective-permute-start
  228.8 6.8 %collective-permute-done = bf16[64,2048]{1,0:T(8,128)(2,1)S(1)} collective-permute-done((bf16[64,2048]{1,0:T(8,128)(2,1)S(1)}, bf16[64,2048]{1,0:T(8,128)(2,1)S(1)}, u32[]{:S(2)}, u32[]{:S(2)}) %collective-permute-start) | collective-permute-done | bytes 262176 | tf_op jit(solution)/shard_map/while/body/eval_jaxpr/ppermute | solution.py:12
  235.7 4.2 convolution_convert_fusion.8
  240.1 16.3 %all-reduce.3.cloned.1.call-done = bf16[64,1024]{1,0:T(8,128)(2,1)} async-done(((bf16[64,1024]{1,0:T(8,128)(2,1)}), bf16[64,1024]{1,0:T(8,128)(2,1)}) %all-reduce.3.cloned.1.call-update) | async-done | bytes 131088 | tf_op jit(solution)/shard_map/while/body/eval_jaxpr/psum | solution.py:59
  256.4 3.9 convolution_convert_fusion.9
  260.3 72.4 %all-reduce.5.cloned.1.call-done = bf16[64,2048]{1,0:T(8,128)(2,1)} async-done(((bf16[64,2048]{1,0:T(8,128)(2,1)}), bf16[64,2048]{1,0:T(8,128)(2,1)}) %all-reduce.5.cloned.1.call-update) | async-done | bytes 262160 | tf_op jit(solution)/shard_map/while/body/eval_jaxpr/psum | solution.py:63
  333.7 1.3 collective-permute-start
  335.2 6.8 %collective-permute-done = bf16[64,2048]{1,0:T(8,128)(2,1)S(1)} collective-permute-done((bf16[64,2048]{1,0:T(8,128)(2,1)S(1)}, bf16[64,2048]{1,0:T(8,128)(2,1)S(1)}, u32[]{:S(2)}, u32[]{:S(2)}) %collective-permute-start) | collective-permute-done | bytes 262176 | tf_op jit(solution)/shard_map/while/body/eval_jaxpr/ppermute | solution.py:12
  342.1 4.2 convolution_convert_fusion.8
  346.4 16.3 %all-reduce.3.cloned.1.call-done = bf16[64,1024]{1,0:T(8,128)(2,1)} async-done(((bf16[64,1024]{1,0:T(8,128)(2,1)}), bf16[64,1024]{1,0:T(8,128)(2,1)}) %all-reduce.3.cloned.1.call-update) | async-done | bytes 131088 | tf_op jit(solution)/shard_map/while/body/eval_jaxpr/psum | solution.py:59
  362.7 3.9 convolution_convert_fusion.9
  366.6 72.4 %all-reduce.5.cloned.1.call-done = bf16[64,2048]{1,0:T(8,128)(2,1)} async-done(((bf16[64,2048]{1,0:T(8,128)(2,1)}), bf16[64,2048]{1,0:T(8,128)(2,1)}) %all-reduce.5.cloned.1.call-update) | async-done | bytes 262160 | tf_op jit(solution)/shard_map/while/body/eval_jaxpr/psum | solution.py:63
  440.1 1.3 collective-permute-start
  441.5 6.8 %collective-permute-done = bf16[64,2048]{1,0:T(8,128)(2,1)S(1)} collective-permute-done((bf16[64,2048]{1,0:T(8,128)(2,1)S(1)}, bf16[64,2048]{1,0:T(8,128)(2,1)S(1)}, u32[]{:S(2)}, u32[]{:S(2)}) %collective-permute-start) | collective-permute-done | bytes 262176 | tf_op jit(solution)/shard_map/while/body/eval_jaxpr/ppermute | solution.py:12
  449.1 1.1 fusion.10
  450.2 8.1 %all_gather.22 = bf16[2,128,1024]{2,1,0:T(8,128)(2,1)S(1)} all-gather(bf16[1,128,1024]{2,1,0:T(8,128)(2,1)S(1)} %fusion.10), channel_id=1, replica_groups=mesh['section'=2,'dp'=8,'mp'=2] {'section'}, dimensions={0}, use_global_device_ids=true | all-gather | bytes 786432 | tf_op jit(solution)/shard_map/all_gather | solution.py:93
  458.3 12.7 %all-gather = bf16[256,1024]{1,0:T(8,128)(2,1)S(1)} all-gather(bf16[128,1024]{1,0:T(8,128)(2,1)S(1)} %get-tuple-element.260), channel_id=2, replica_groups=mesh['section'=2,'dp'=8,'mp'=2] {'section'}, dimensions={0}, use_global_device_ids=true | all-gather | bytes 786432 | tf_op jit(solution)/shard_map/all_gather | solution.py:92
  471.1 3.3 all-gather.11.cloned.1.call-done
  474.4 1.8 convolution_convert_fusion.4
  476.2 1.8 convolution_convert_fusion.5
  478.0 2.8 add_bitcast_fusion.1
  480.8 15.6 %all-gather.13.cloned.1.call-done = bf16[256,2048]{1,0:T(8,128)(2,1)} async-done(((bf16[128,2048]{1,0:T(8,128)(2,1)}), bf16[256,2048]{1,0:T(8,128)(2,1)}) %all-gather.13.cloned.1.call-update) | async-done | bytes 1048592 | tf_op jit(solution)/shard_map/all_gather | solution.py:91
  496.4 1.8 convolution_convert_fusion.2
  498.1 1.8 convolution_convert_fusion.3
  499.9 2.8 add_bitcast_fusion
  (49 shorter events, 6.7 us)
Async XLA Ops:
  7.2 120.3 %copy-start.4 = (bf16[128,2048]{1,0:T(8,128)(2,1)S(1)}, bf16[128,2048]{1,0:T(8,128)(2,1)}, u32[]{:S(2)}) copy-start(bf16[128,2048]{1,0:T(8,128)(2,1)} %param.9) | copy-start | bytes 1572868
  7.2 120.3 %copy-start.2 = (bf16[1,128,1024]{2,1,0:T(8,128)(2,1)S(1)}, bf16[1,128,1024]{2,1,0:T(8,128)(2,1)}, u32[]{:S(2)}) copy-start(bf16[1,128,1024]{2,1,0:T(8,128)(2,1)} %param.8) | copy-start | bytes 786436
  7.2 61.8 %all-gather.7.cloned.1.call-start = ((), (), s32[]{:S(2)}) async-start(), calls=%async_computation | async-start | bytes 6291456 | tf_op jit(solution)/shard_map/all_gather | solution.py:39
  7.9 119.4 %all-gather.9.cloned.1.call-start = ((), (), s32[]{:S(2)}) async-start(), calls=%async_computation.1 | async-start | bytes 6291456 | tf_op jit(solution)/shard_map/all_gather | solution.py:38
  127.5 22.5 %all-reduce.3.cloned.1.call-start = ((), (), s32[]{:S(2)}) async-start(), calls=%async_computation.4 | async-start | bytes 262144 | tf_op jit(solution)/shard_map/while/body/eval_jaxpr/psum | solution.py:59
  132.0 94.3 %all-reduce.5.cloned.1.call-start = ((), (), s32[]{:S(2)}) async-start(), calls=%async_computation.5 | async-start | bytes 524288 | tf_op jit(solution)/shard_map/while/body/eval_jaxpr/psum | solution.py:63
  150.0 78.6 %copy-start = (bf16[64,1024]{1,0:T(8,128)(2,1)S(1)}, bf16[64,1024]{1,0:T(8,128)(2,1)}, u32[]{:S(2)}) copy-start(bf16[64,1024]{1,0:T(8,128)(2,1)} %all-reduce.3.cloned.1.call-done) | copy-start | bytes 393220 | tf_op jit(solution)/shard_map/while
  227.3 8.3 %collective-permute-start = (bf16[64,2048]{1,0:T(8,128)(2,1)S(1)}, bf16[64,2048]{1,0:T(8,128)(2,1)S(1)}, u32[]{:S(2)}, u32[]{:S(2)}) collective-permute-start(bf16[64,2048]{1,0:T(8,128)(2,1)S(1)} %get-tuple-element.364), channel_id=1, source_target_pairs={{16,0},{17,1},{18,2},{19,3},{20,4},{21,5},{22,6},{23,7},{24,8},{25... | collective-permute-start | bytes 786440 | tf_op jit(solution)/shard_map/while/body/eval_jaxpr/ppermute | solution.py:12
  235.6 20.8 %all-reduce.3.cloned.1.call-start = ((), (), s32[]{:S(2)}) async-start(), calls=%async_computation.4 | async-start | bytes 262144 | tf_op jit(solution)/shard_map/while/body/eval_jaxpr/psum | solution.py:59
  240.0 92.6 %all-reduce.5.cloned.1.call-start = ((), (), s32[]{:S(2)}) async-start(), calls=%async_computation.5 | async-start | bytes 524288 | tf_op jit(solution)/shard_map/while/body/eval_jaxpr/psum | solution.py:63
  256.4 78.6 %copy-start = (bf16[64,1024]{1,0:T(8,128)(2,1)S(1)}, bf16[64,1024]{1,0:T(8,128)(2,1)}, u32[]{:S(2)}) copy-start(bf16[64,1024]{1,0:T(8,128)(2,1)} %all-reduce.3.cloned.1.call-done) | copy-start | bytes 393220 | tf_op jit(solution)/shard_map/while
  333.7 8.3 %collective-permute-start = (bf16[64,2048]{1,0:T(8,128)(2,1)S(1)}, bf16[64,2048]{1,0:T(8,128)(2,1)S(1)}, u32[]{:S(2)}, u32[]{:S(2)}) collective-permute-start(bf16[64,2048]{1,0:T(8,128)(2,1)S(1)} %get-tuple-element.364), channel_id=1, source_target_pairs={{16,0},{17,1},{18,2},{19,3},{20,4},{21,5},{22,6},{23,7},{24,8},{25... | collective-permute-start | bytes 786440 | tf_op jit(solution)/shard_map/while/body/eval_jaxpr/ppermute | solution.py:12
  342.0 20.8 %all-reduce.3.cloned.1.call-start = ((), (), s32[]{:S(2)}) async-start(), calls=%async_computation.4 | async-start | bytes 262144 | tf_op jit(solution)/shard_map/while/body/eval_jaxpr/psum | solution.py:59
  346.4 92.6 %all-reduce.5.cloned.1.call-start = ((), (), s32[]{:S(2)}) async-start(), calls=%async_computation.5 | async-start | bytes 524288 | tf_op jit(solution)/shard_map/while/body/eval_jaxpr/psum | solution.py:63
  362.7 78.6 %copy-start = (bf16[64,1024]{1,0:T(8,128)(2,1)S(1)}, bf16[64,1024]{1,0:T(8,128)(2,1)}, u32[]{:S(2)}) copy-start(bf16[64,1024]{1,0:T(8,128)(2,1)} %all-reduce.3.cloned.1.call-done) | copy-start | bytes 393220 | tf_op jit(solution)/shard_map/while
  440.1 8.3 %collective-permute-start = (bf16[64,2048]{1,0:T(8,128)(2,1)S(1)}, bf16[64,2048]{1,0:T(8,128)(2,1)S(1)}, u32[]{:S(2)}, u32[]{:S(2)}) collective-permute-start(bf16[64,2048]{1,0:T(8,128)(2,1)S(1)} %get-tuple-element.364), channel_id=1, source_target_pairs={{16,0},{17,1},{18,2},{19,3},{20,4},{21,5},{22,6},{23,7},{24,8},{25... | collective-permute-start | bytes 786440 | tf_op jit(solution)/shard_map/while/body/eval_jaxpr/ppermute | solution.py:12
  448.3 22.7 %copy-start.1 = (bf16[128,2048]{1,0:T(8,128)(2,1)}, bf16[128,2048]{1,0:T(8,128)(2,1)S(1)}, u32[]{:S(2)}) copy-start(bf16[128,2048]{1,0:T(8,128)(2,1)S(1)} %get-tuple-element.261) | copy-start | bytes 1572868
  448.3 29.6 %copy-start.3 = (bf16[128,2048]{1,0:T(8,128)(2,1)}, bf16[128,2048]{1,0:T(8,128)(2,1)S(1)}, u32[]{:S(2)}) copy-start(bf16[128,2048]{1,0:T(8,128)(2,1)S(1)} %get-tuple-element.259) | copy-start | bytes 1572868
  448.3 26.1 %all-gather.11.cloned.1.call-start = ((), (), s32[]{:S(2)}) async-start(), calls=%async_computation.2 | async-start | bytes 1572864 | tf_op jit(solution)/shard_map/all_gather | solution.py:90
  449.1 47.3 %all-gather.13.cloned.1.call-start = ((), (), s32[]{:S(2)}) async-start(), calls=%async_computation.3 | async-start | bytes 1572864 | tf_op jit(solution)/shard_map/all_gather | solution.py:91
Sparse Core Ops, SparseCore 0:
  9.5 59.4 all-gather.6
  70.6 56.7 all-gather.8
  132.1 17.8 all-reduce.2
  154.0 72.1 all-reduce.4
  240.1 16.1 all-reduce.2
  260.4 72.2 all-reduce.4
  346.5 16.1 all-reduce.2
  366.7 72.2 all-reduce.4
  450.7 23.6 all-gather.10
  476.4 19.9 all-gather.12
where the time goes:
time: 510 us
  waiting for transfers between devices  428 us (84%)
  matrix products  31.4 us (6%)
  blocking collectives  20.7 us (4%)
  between operations  14.2 us (3%)
  other arithmetic  10.8 us (2%)
    psum x3, waiting for transfers between devices, advance(): total = lax.psum(branch.astype(jnp.bfloat16), 'dp').astype(jnp.float32)  217 us
    all_gather x1, waiting for transfers between devices, body(): lax.all_gather(w_out, 'section', axis=1, tiled=True)  60.3 us
    all_gather x1, waiting for transfers between devices, body(): lax.all_gather(w_in, 'section', axis=1, tiled=True)  58.3 us
    psum x3, waiting for transfers between devices, advance(): lax.psum(partial_value.astype(jnp.bfloat16), 'mp').astype(jnp.float32)  50.6 us
    ppermute x3, waiting for transfers between devices, shifted(): return lax.ppermute(value, axis, pairs)  20.4 us
    all_gather x1, waiting for transfers between devices, body(): lax.all_gather(dys[None], 'section', axis=0, tiled=True)  15.6 us
    dot_general x3, matrix products, advance(): lax.dot_general(upper, out_rows, (((1,), (1,)), ((), ())), preferred_elem...  12.7 us
    all_gather x1, blocking collectives, body(): lax.all_gather(gees[None], 'section', axis=0, tiled=True)  12.7 us
  transfers between devices with their start and end apart: 13, of which 13 were waited for; matrix products, arithmetic and copies ran while one was open for 2% of the time, Pallas kernels for 0%

commit v1 on v0

--- a/solution.py
+++ b/solution.py
@@ -4,6 +4,29 @@
 from jax.sharding import PartitionSpec as P
 
 MICRO = 2
+
+
+def in_order(tiles, dim):
+    tiles = jnp.moveaxis(tiles, 0, dim)
+    lengths = tiles.shape
+    return tiles.reshape(*lengths[:dim], lengths[dim] * lengths[dim + 1], *lengths[dim + 2 :])
+
+
+def doubled(value, axis):
+    size, index = (lax.axis_size(axis), lax.axis_index(axis))
+    tiles, distance = (value[None], 1)
+    while distance < size:
+        partner_block = lax.ppermute(tiles, axis, [(i, i ^ distance) for i in range(size)])
+        low = index & distance == 0
+        tiles = jnp.concatenate(
+            [jnp.where(low, tiles, partner_block), jnp.where(low, partner_block, tiles)]
+        )
+        distance *= 2
+    return tiles
+
+
+def collect(x, axis, dim):
+    return in_order(doubled(x, axis), dim)
 
 
 def shifted(value, axis, by):
@@ -35,7 +58,7 @@
     block = tok_rows // MICRO
     width = out_grad.shape[1]
     full_in, full_out = (
-        lax.all_gather(w_in, "section", axis=1, tiled=True),
+        collect(w_in, "section", 1),
         lax.all_gather(w_out, "section", axis=1, tiled=True),
     )
     units = full_in.shape[1] * full_in.shape[2]

time: 510 us -> 486 us (0.953)
  waiting for transfers between devices: 428 us -> 397 us
    ppermute x0 -> x1, waiting for transfers between devices: none -> 80.7 us  [doubled(): lax.ppermute(tiles, axis, [(i, i ^ distance) for i in range(size)])]
    all_gather x1 -> x0, waiting for transfers between devices: 58.3 us -> none  [body(): lax.all_gather(w_in, 'section', axis=1, tiled=True)]
    all_gather x1, waiting for transfers between devices: 60.3 us -> 6.07 us  [body(): lax.all_gather(w_out, 'section', axis=1, tiled=True)]
  transfers between devices with their start and end apart: 13 -> 13, of which waited for: 13 -> 13; matrix products, arithmetic and copies ran while one was open for 2% -> 3% of each run, Pallas kernels for 0% -> 0%
where the time goes in v1:
time: 486 us
  waiting for transfers between devices  397 us (82%)
  matrix products  31.4 us (6%)
  blocking collectives  20.7 us (4%)
  other arithmetic  15 us (3%)
  between operations  13.9 us (3%)
  starting transfers between devices  7.17 us (1%)
    psum x3, waiting for transfers between devices, advance(): total = lax.psum(branch.astype(jnp.bfloat16), 'dp').astype(jnp.float32)  217 us
    ppermute x1, waiting for transfers between devices, doubled(): lax.ppermute(tiles, axis, [(i, i ^ distance) for i in range(size)])  80.7 us
    psum x3, waiting for transfers between devices, advance(): lax.psum(partial_value.astype(jnp.bfloat16), 'mp').astype(jnp.float32)  52.1 us
    ppermute x3, waiting for transfers between devices, shifted(): return lax.ppermute(value, axis, pairs)  20.4 us
    all_gather x1, waiting for transfers between devices, body(): lax.all_gather(dys[None], 'section', axis=0, tiled=True)  15.7 us
    dot_general x3, matrix products, advance(): lax.dot_general(upper, out_rows, (((1,), (1,)), ((), ())), preferred_elem...  12.7 us
    all_gather x1, blocking collectives, body(): lax.all_gather(gees[None], 'section', axis=0, tiled=True)  12.7 us
    dot_general x3, matrix products, advance(): branch = jnp.dot(gee, in_rows, preferred_element_type=jnp.float32)  11.6 us
  transfers between devices with their start and end apart: 13, of which 13 were waited for; matrix products, arithmetic and copies ran while one was open for 3% of the time, Pallas kernels for 0%

profile of v1, /device:TPU:0, one launch (start us, length us, event | category | flops | bytes accessed | tf_op | source)
XLA Modules:
  0.0 485.6 jit_solution(8040776396674954654)
XLA Ops:
  7.9 3.0 collective-permute-start.1
  10.9 80.7 %collective-permute-done.1 = bf16[1,1,1,512,2048]{4,3,2,1,0:T(8,128)(2,1)S(1)} collective-permute-done((bf16[1,1,1,512,2048]{4,3,2,1,0:T(8,128)(2,1)}, bf16[1,1,1,512,2048]{4,3,2,1,0:T(8,128)(2,1)S(1)}, u32[]{:S(2)}, u32[]{:S(2)}) %collective-permute-start.1) | collective-permute-done | bytes 2097184 | tf_op jit(solution)/shard_map/ppermute | solution.py:19
  91.6 1.9 broadcast_select_fusion.1
  93.5 2.4 pad_maximum_fusion
  95.9 6.1 %all-gather.6.cloned.1.call-done = bf16[1,2,512,2048]{3,2,0,1:T(8,128)(2,1)} async-done(((bf16[1,1,512,2048]{3,2,0,1:T(8,128)(2,1)}), bf16[1,2,512,2048]{3,2,0,1:T(8,128)(2,1)}) %all-gather.6.cloned.1.call-update) | async-done | bytes 4194320 | tf_op jit(solution)/shard_map/all_gather | solution.py:62
  102.1 322.3 %while.21 = (s32[]{:T(128)}, bf16[64,2048]{1,0:T(8,128)(2,1)S(1)}, bf16[128,2048]{1,0:T(8,128)(2,1)S(1)}, bf16[128,1024]{1,0:T(8,128)(2,1)S(1)}, bf16[128,2048]{...) while((s32[]{:T(128)}, bf16[64,2048]{1,0:T(8,128)(2,1)S(1)}, ...), condition=%wide.region_3.4_spmd, body=%wide.region_0.3_spmd.sunk | while | flops 539820032 | bytes 16384420 | solution.py:105
  102.4 4.2 convolution_convert_fusion.8
  106.7 19.5 %all-reduce.3.cloned.1.call-done = bf16[64,1024]{1,0:T(8,128)(2,1)} async-done(((bf16[64,1024]{1,0:T(8,128)(2,1)}), bf16[64,1024]{1,0:T(8,128)(2,1)}) %all-reduce.3.cloned.1.call-update) | async-done | bytes 131088 | tf_op jit(solution)/shard_map/while/body/eval_jaxpr/psum | solution.py:82
  126.2 3.9 convolution_convert_fusion.9
  130.1 72.4 %all-reduce.5.cloned.1.call-done = bf16[64,2048]{1,0:T(8,128)(2,1)} async-done(((bf16[64,2048]{1,0:T(8,128)(2,1)}), bf16[64,2048]{1,0:T(8,128)(2,1)}) %all-reduce.5.cloned.1.call-update) | async-done | bytes 262160 | tf_op jit(solution)/shard_map/while/body/eval_jaxpr/psum | solution.py:86
  203.5 1.3 collective-permute-start
  205.0 6.8 %collective-permute-done = bf16[64,2048]{1,0:T(8,128)(2,1)S(1)} collective-permute-done((bf16[64,2048]{1,0:T(8,128)(2,1)S(1)}, bf16[64,2048]{1,0:T(8,128)(2,1)S(1)}, u32[]{:S(2)}, u32[]{:S(2)}) %collective-permute-start) | collective-permute-done | bytes 262176 | tf_op jit(solution)/shard_map/while/body/eval_jaxpr/ppermute | solution.py:35
  211.9 4.2 convolution_convert_fusion.8
  216.2 16.3 %all-reduce.3.cloned.1.call-done = bf16[64,1024]{1,0:T(8,128)(2,1)} async-done(((bf16[64,1024]{1,0:T(8,128)(2,1)}), bf16[64,1024]{1,0:T(8,128)(2,1)}) %all-reduce.3.cloned.1.call-update) | async-done | bytes 131088 | tf_op jit(solution)/shard_map/while/body/eval_jaxpr/psum | solution.py:82
  232.5 3.9 convolution_convert_fusion.9
  236.4 72.4 %all-reduce.5.cloned.1.call-done = bf16[64,2048]{1,0:T(8,128)(2,1)} async-done(((bf16[64,2048]{1,0:T(8,128)(2,1)}), bf16[64,2048]{1,0:T(8,128)(2,1)}) %all-reduce.5.cloned.1.call-update) | async-done | bytes 262160 | tf_op jit(solution)/shard_map/while/body/eval_jaxpr/psum | solution.py:86
  311.3 6.8 %collective-permute-done = bf16[64,2048]{1,0:T(8,128)(2,1)S(1)} collective-permute-done((bf16[64,2048]{1,0:T(8,128)(2,1)S(1)}, bf16[64,2048]{1,0:T(8,128)(2,1)S(1)}, u32[]{:S(2)}, u32[]{:S(2)}) %collective-permute-start) | collective-permute-done | bytes 262176 | tf_op jit(solution)/shard_map/while/body/eval_jaxpr/ppermute | solution.py:35
  318.2 4.2 convolution_convert_fusion.8
  322.6 16.3 %all-reduce.3.cloned.1.call-done = bf16[64,1024]{1,0:T(8,128)(2,1)} async-done(((bf16[64,1024]{1,0:T(8,128)(2,1)}), bf16[64,1024]{1,0:T(8,128)(2,1)}) %all-reduce.3.cloned.1.call-update) | async-done | bytes 131088 | tf_op jit(solution)/shard_map/while/body/eval_jaxpr/psum | solution.py:82
  338.9 3.9 convolution_convert_fusion.9
  342.8 72.4 %all-reduce.5.cloned.1.call-done = bf16[64,2048]{1,0:T(8,128)(2,1)} async-done(((bf16[64,2048]{1,0:T(8,128)(2,1)}), bf16[64,2048]{1,0:T(8,128)(2,1)}) %all-reduce.5.cloned.1.call-update) | async-done | bytes 262160 | tf_op jit(solution)/shard_map/while/body/eval_jaxpr/psum | solution.py:86
  417.7 6.8 %collective-permute-done = bf16[64,2048]{1,0:T(8,128)(2,1)S(1)} collective-permute-done((bf16[64,2048]{1,0:T(8,128)(2,1)S(1)}, bf16[64,2048]{1,0:T(8,128)(2,1)S(1)}, u32[]{:S(2)}, u32[]{:S(2)}) %collective-permute-start) | collective-permute-done | bytes 262176 | tf_op jit(solution)/shard_map/while/body/eval_jaxpr/ppermute | solution.py:35
  426.4 8.1 %all_gather.18 = bf16[2,128,1024]{2,1,0:T(8,128)(2,1)S(1)} all-gather(bf16[1,128,1024]{2,1,0:T(8,128)(2,1)S(1)} %fusion.10), channel_id=1, replica_groups=mesh['section'=2,'dp'=8,'mp'=2] {'section'}, dimensions={0}, use_global_device_ids=true | all-gather | bytes 786432 | tf_op jit(solution)/shard_map/all_gather | solution.py:116
  434.5 12.7 %all-gather = bf16[256,1024]{1,0:T(8,128)(2,1)S(1)} all-gather(bf16[128,1024]{1,0:T(8,128)(2,1)S(1)} %get-tuple-element.260), channel_id=2, replica_groups=mesh['section'=2,'dp'=8,'mp'=2] {'section'}, dimensions={0}, use_global_device_ids=true | all-gather | bytes 786432 | tf_op jit(solution)/shard_map/all_gather | solution.py:115
  447.2 3.3 all-gather.8.cloned.1.call-done
  450.5 1.8 convolution_convert_fusion.5
  452.3 1.8 convolution_convert_fusion.4
  454.1 2.8 add_bitcast_fusion.1
  456.9 15.7 %all-gather.10.cloned.1.call-done = bf16[256,2048]{1,0:T(8,128)(2,1)} async-done(((bf16[128,2048]{1,0:T(8,128)(2,1)}), bf16[256,2048]{1,0:T(8,128)(2,1)}) %all-gather.10.cloned.1.call-update) | async-done | bytes 1048592 | tf_op jit(solution)/shard_map/all_gather | solution.py:114
  472.7 1.8 convolution_convert_fusion.3
  474.4 1.8 convolution_convert_fusion.2
  476.2 2.8 add_bitcast_fusion
  (50 shorter events, 9.7 us)
Async XLA Ops:
  7.2 94.8 %all-gather.6.cloned.1.call-start = ((), (), s32[]{:S(2)}) async-start(), calls=%async_computation | async-start | bytes 6291456 | tf_op jit(solution)/shard_map/all_gather | solution.py:62
  7.9 83.7 %collective-permute-start.1 = (bf16[1,1,1,512,2048]{4,3,2,1,0:T(8,128)(2,1)}, bf16[1,1,1,512,2048]{4,3,2,1,0:T(8,128)(2,1)S(1)}, u32[]{:S(2)}, u32[]{:S(2)}) collective-permute-start(bf16[1,1,1,512,2048]{4,3,2,1,0:T(8,128)(2,1)} %bitcast.39), channel_id=1, source_target_pairs={{0,16},{16,0},{1,17},{17,1},{2,18},{18,2},{3,19},{19,3},{4,20},{20... | collective-permute-start | bytes 6291464 | tf_op jit(solution)/shard_map/ppermute | solution.py:19
  93.5 8.6 %copy-start.2 = (bf16[1,128,1024]{2,1,0:T(8,128)(2,1)S(1)}, bf16[1,128,1024]{2,1,0:T(8,128)(2,1)}, u32[]{:S(2)}) copy-start(bf16[1,128,1024]{2,1,0:T(8,128)(2,1)} %param.8) | copy-start | bytes 786436
  93.5 8.6 %copy-start.4 = (bf16[128,2048]{1,0:T(8,128)(2,1)S(1)}, bf16[128,2048]{1,0:T(8,128)(2,1)}, u32[]{:S(2)}) copy-start(bf16[128,2048]{1,0:T(8,128)(2,1)} %param.9) | copy-start | bytes 1572868
  102.2 24.0 %all-reduce.3.cloned.1.call-start = ((), (), s32[]{:S(2)}) async-start(), calls=%async_computation.3 | async-start | bytes 262144 | tf_op jit(solution)/shard_map/while/body/eval_jaxpr/psum | solution.py:82
  106.6 95.8 %all-reduce.5.cloned.1.call-start = ((), (), s32[]{:S(2)}) async-start(), calls=%async_computation.4 | async-start | bytes 524288 | tf_op jit(solution)/shard_map/while/body/eval_jaxpr/psum | solution.py:86
  126.2 78.6 %copy-start = (bf16[64,1024]{1,0:T(8,128)(2,1)S(1)}, bf16[64,1024]{1,0:T(8,128)(2,1)}, u32[]{:S(2)}) copy-start(bf16[64,1024]{1,0:T(8,128)(2,1)} %all-reduce.3.cloned.1.call-done) | copy-start | bytes 393220 | tf_op jit(solution)/shard_map/while
  203.5 8.3 %collective-permute-start = (bf16[64,2048]{1,0:T(8,128)(2,1)S(1)}, bf16[64,2048]{1,0:T(8,128)(2,1)S(1)}, u32[]{:S(2)}, u32[]{:S(2)}) collective-permute-start(bf16[64,2048]{1,0:T(8,128)(2,1)S(1)} %get-tuple-element.366), channel_id=1, source_target_pairs={{16,0},{17,1},{18,2},{19,3},{20,4},{21,5},{22,6},{23,7},{24,8},{25... | collective-permute-start | bytes 786440 | tf_op jit(solution)/shard_map/while/body/eval_jaxpr/ppermute | solution.py:35
  211.8 20.8 %all-reduce.3.cloned.1.call-start = ((), (), s32[]{:S(2)}) async-start(), calls=%async_computation.3 | async-start | bytes 262144 | tf_op jit(solution)/shard_map/while/body/eval_jaxpr/psum | solution.py:82
  216.2 92.6 %all-reduce.5.cloned.1.call-start = ((), (), s32[]{:S(2)}) async-start(), calls=%async_computation.4 | async-start | bytes 524288 | tf_op jit(solution)/shard_map/while/body/eval_jaxpr/psum | solution.py:86
  232.5 78.6 %copy-start = (bf16[64,1024]{1,0:T(8,128)(2,1)S(1)}, bf16[64,1024]{1,0:T(8,128)(2,1)}, u32[]{:S(2)}) copy-start(bf16[64,1024]{1,0:T(8,128)(2,1)} %all-reduce.3.cloned.1.call-done) | copy-start | bytes 393220 | tf_op jit(solution)/shard_map/while
  309.8 8.3 %collective-permute-start = (bf16[64,2048]{1,0:T(8,128)(2,1)S(1)}, bf16[64,2048]{1,0:T(8,128)(2,1)S(1)}, u32[]{:S(2)}, u32[]{:S(2)}) collective-permute-start(bf16[64,2048]{1,0:T(8,128)(2,1)S(1)} %get-tuple-element.366), channel_id=1, source_target_pairs={{16,0},{17,1},{18,2},{19,3},{20,4},{21,5},{22,6},{23,7},{24,8},{25... | collective-permute-start | bytes 786440 | tf_op jit(solution)/shard_map/while/body/eval_jaxpr/ppermute | solution.py:35
  318.1 20.8 %all-reduce.3.cloned.1.call-start = ((), (), s32[]{:S(2)}) async-start(), calls=%async_computation.3 | async-start | bytes 262144 | tf_op jit(solution)/shard_map/while/body/eval_jaxpr/psum | solution.py:82
  322.5 92.6 %all-reduce.5.cloned.1.call-start = ((), (), s32[]{:S(2)}) async-start(), calls=%async_computation.4 | async-start | bytes 524288 | tf_op jit(solution)/shard_map/while/body/eval_jaxpr/psum | solution.py:86
  338.9 78.6 %copy-start = (bf16[64,1024]{1,0:T(8,128)(2,1)S(1)}, bf16[64,1024]{1,0:T(8,128)(2,1)}, u32[]{:S(2)}) copy-start(bf16[64,1024]{1,0:T(8,128)(2,1)} %all-reduce.3.cloned.1.call-done) | copy-start | bytes 393220 | tf_op jit(solution)/shard_map/while
  416.2 8.3 %collective-permute-start = (bf16[64,2048]{1,0:T(8,128)(2,1)S(1)}, bf16[64,2048]{1,0:T(8,128)(2,1)S(1)}, u32[]{:S(2)}, u32[]{:S(2)}) collective-permute-start(bf16[64,2048]{1,0:T(8,128)(2,1)S(1)} %get-tuple-element.366), channel_id=1, source_target_pairs={{16,0},{17,1},{18,2},{19,3},{20,4},{21,5},{22,6},{23,7},{24,8},{25... | collective-permute-start | bytes 786440 | tf_op jit(solution)/shard_map/while/body/eval_jaxpr/ppermute | solution.py:35
  424.5 22.7 %copy-start.1 = (bf16[128,2048]{1,0:T(8,128)(2,1)}, bf16[128,2048]{1,0:T(8,128)(2,1)S(1)}, u32[]{:S(2)}) copy-start(bf16[128,2048]{1,0:T(8,128)(2,1)S(1)} %get-tuple-element.261) | copy-start | bytes 1572868
  424.5 29.6 %copy-start.3 = (bf16[128,2048]{1,0:T(8,128)(2,1)}, bf16[128,2048]{1,0:T(8,128)(2,1)S(1)}, u32[]{:S(2)}) copy-start(bf16[128,2048]{1,0:T(8,128)(2,1)S(1)} %get-tuple-element.259) | copy-start | bytes 1572868
  424.5 26.1 %all-gather.8.cloned.1.call-start = ((), (), s32[]{:S(2)}) async-start(), calls=%async_computation.1 | async-start | bytes 1572864 | tf_op jit(solution)/shard_map/all_gather | solution.py:113
  425.2 47.5 %all-gather.10.cloned.1.call-start = ((), (), s32[]{:S(2)}) async-start(), calls=%async_computation.2 | async-start | bytes 1572864 | tf_op jit(solution)/shard_map/all_gather | solution.py:114
Sparse Core Ops, SparseCore 0:
  9.5 92.4 all-gather.5
  106.7 19.4 all-reduce.2
  130.2 72.2 all-reduce.4
  216.3 16.1 all-reduce.2
  236.5 72.1 all-reduce.4
  322.6 16.1 all-reduce.2
  342.9 72.2 all-reduce.4
  426.8 23.6 all-gather.7
  452.7 19.9 all-gather.9
